TPU v7x, 128 devices: a whole 4x4x4 slice. The times are simulated.
128 devices in a mesh: graph: 128 (over z, y, x, core).
Axes of the slice: x: 4, y: 4, z: 4, core: 2. Of those that a mesh axis runs over, the one named last changes fastest.
Arguments:
- node_feats: bfloat16 [524288, 100], P('graph')
- w_one: float32 [100, 256], replicated
- w_two: float32 [256, 47], replicated
- send_idx: int32 [256, 1024], P('graph')
- edge_src: int32 [524288, 4], P('graph')
- edge_w: float32 [524288, 4], P('graph')
- halo_src: int32 [131072, 4], P('graph')
- halo_w: float32 [131072, 4], P('graph')
- labels: int32 [524288], P('graph')
- label_mask: int32 [524288], P('graph')
Outputs:
- output 1: float32 [], replicated
- output 2: float32 [100, 256], replicated
- output 3: float32 [256, 47], replicated
All inputs are finite; a program needn't handle non-finite values.
Results may differ from a plain program's by a relative error of at most 0.001.
Values are sent between devices in bfloat16 or wider.
A program may use at most 1 GiB of HBM per device.

v0:
```python
import jax
import jax.numpy as jnp
from jax import lax
from jax.sharding import PartitionSpec as P


def gather_sum(buffer, src_rows, weights):
    return jnp.sum(buffer[src_rows] * weights[:, :, None], axis=1)


def head_grads(z_two, logits, labels, label_mask, w_two_b):
    onehot = (lax.broadcasted_iota(jnp.int32, logits.shape, 1) == labels[:, None]).astype(jnp.float32)
    mark_rows = label_mask.astype(jnp.float32)
    label_count = lax.psum(jnp.sum(mark_rows), 'graph')
    log_norm = jax.nn.logsumexp(logits, axis=1)
    loss_value = lax.psum(jnp.sum(mark_rows * (log_norm - jnp.sum(logits * onehot, axis=1))), 'graph') / label_count
    grad_logits = ((jax.nn.softmax(logits, axis=1) - onehot) * (mark_rows / label_count)[:, None]).astype(jnp.bfloat16)
    grad_two = lax.psum(jnp.einsum('nh,nc->hc', z_two, grad_logits, preferred_element_type=jnp.float32), 'graph')
    grad_agg = jnp.einsum('nc,hc->nh', grad_logits, w_two_b, preferred_element_type=jnp.float32)
    return loss_value, grad_two, grad_agg


def solution(mesh):
    num_parts = mesh.shape['graph']
    to_next = [(dev_id, (dev_id + 1) % num_parts) for dev_id in range(num_parts)]
    to_prev = [(dev_id, (dev_id - 1) % num_parts) for dev_id in range(num_parts)]
    row_spec = P('graph', None)

    def exchange(node_rows, send_idx, halo_rows):
        from_prev = lax.ppermute(node_rows[send_idx[0, :halo_rows]], 'graph', to_next)
        from_next = lax.ppermute(node_rows[send_idx[1, :halo_rows]], 'graph', to_prev)
        return jnp.concatenate([node_rows, from_next, from_prev], axis=0)

    def device_step(node_feats, w_one, w_two, send_idx, edge_src, edge_w, labels, label_mask):
        own_rows = node_feats.shape[0]
        halo_rows = send_idx.shape[1] // 2
        w_one_b = w_one.astype(jnp.bfloat16)
        w_two_b = w_two.astype(jnp.bfloat16)
        z_one = gather_sum(exchange(node_feats, send_idx, halo_rows), edge_src, edge_w).astype(jnp.bfloat16)
        y_one = jnp.dot(z_one, w_one_b, preferred_element_type=jnp.float32)
        h_two = jnp.maximum(y_one, 0.0).astype(jnp.bfloat16)
        z_two = gather_sum(exchange(h_two, send_idx, halo_rows), edge_src, edge_w).astype(jnp.bfloat16)
        logits = jnp.dot(z_two, w_two_b, preferred_element_type=jnp.float32)
        loss_value, grad_two, grad_agg = head_grads(z_two, logits, labels, label_mask, w_two_b)
        contrib = (edge_w[:, :, None] * grad_agg[:, None, :]).reshape(-1, grad_agg.shape[1])
        grad_buf = jax.ops.segment_sum(contrib, edge_src.reshape(-1), num_segments=own_rows + 2 * halo_rows)
        back_prev = lax.ppermute(grad_buf[own_rows:own_rows + halo_rows], 'graph', to_next)
        back_next = lax.ppermute(grad_buf[own_rows + halo_rows:], 'graph', to_prev)
        grad_hidden = grad_buf[:own_rows].at[send_idx[0, :halo_rows]].add(back_next).at[send_idx[1, :halo_rows]].add(back_prev)
        grad_pre = jnp.where(y_one > 0, grad_hidden, 0.0).astype(jnp.bfloat16)
        grad_one = lax.psum(jnp.einsum('nf,nh->fh', z_one, grad_pre, preferred_element_type=jnp.float32), 'graph')
        return loss_value, grad_one, grad_two

    mapped = jax.shard_map(device_step, mesh=mesh, in_specs=(row_spec, P(), P(), row_spec, row_spec, row_spec, P('graph'), P('graph')), out_specs=(P(), P(), P()), check_vma=False)

    def program(node_feats, w_one, w_two, send_idx, edge_src, edge_w, halo_src, halo_w, labels, label_mask):
        return mapped(node_feats, w_one, w_two, send_idx, edge_src, edge_w, labels, label_mask)

    return program
```

profile of v0, /device:TPU:1, one launch (start us, length us, event | category | flops | bytes accessed | tf_op | source)
XLA Modules:
  0.0 623.4 jit_solution(13653123380049438623)
XLA Ops:
  7.2 0.0 copy-start.8
  7.2 0.0 all-reduce.3.cloned.1.call-start
  7.2 0.8 compare_select_fusion.2
  8.0 0.0 copy-start.12
  8.0 1.6 copy.18
  9.7 1.9 gather_fusion
  11.6 1.4 collective-permute-start
  12.9 1.9 gather_fusion.1
  14.8 1.3 collective-permute-start.1
  16.1 0.0 copy-done.8
  16.1 0.6 copy.19
  16.8 1.6 reshape.93
  18.4 0.0 copy-done.12
  18.4 0.6 copy.20
  19.1 0.0 collective-permute-done
  19.1 4.8 collective-permute-done.1
  23.9 1.6 pad_maximum_fusion.1
  25.5 57.4 %gather_fusion.2 = bf16[16384,100]{1,0:T(8,128)(2,1)} fusion(bf16[5120,100]{1,0:T(8,128)(2,1)S(1)} %pad_maximum_fusion.1, s32[16384]{0:T(1024)S(1)} %broadcast_clamp_fusion), kind=kCustom, calls=%fused_computation.2 | custom fusion | bytes 6619136 | tf_op jit(solution)/shard_map/gather | solution.py:8
  82.9 23.6 %fusion.2 = bf16[4096,100]{1,0:T(8,128)(2,1)S(1)} fusion(bf16[4096,4,100]{2,1,0:T(4,128)(2,1)} %bitcast.12, f32[4096,4]{1,0:T(8,128)S(1)} %copy.20), kind=kLoop, calls=%fused_computation.13 | loop fusion | flops 4505600 | bytes 4161536 | tf_op jit(solution)/shard_map/reduce_sum | solution.py:8
  106.6 3.2 maximum_convert_fusion
  109.8 4.0 gather_fusion.4
  113.8 0.0 copy-done.3
  113.9 4.1 gather_fusion.3
  117.9 9.0 %collective-permute-start.2 = (bf16[512,256]{1,0:T(8,128)(2,1)}, bf16[512,256]{1,0:T(8,128)(2,1)}, u32[]{:S(2)}, u32[]{:S(2)}) collective-permute-start(bf16[512,256]{1,0:T(8,128)(2,1)} %gather_fusion.3), channel_id=1, source_target_pairs={{0,127},{1,0},{2,1},{3,2},{4,3},{5,4},{6,5},{7,6},{8,7},{9,8},{10,... | collective-permute-start | bytes 786440 | tf_op jit(solution)/shard_map/ppermute | solution.py:31
  126.9 0.0 collective-permute-start.3
  127.0 0.0 copy-done
  127.0 1.6 mul.54
  128.6 1.5 copy.22
  130.1 1.6 reshape.125
  131.7 0.0 collective-permute-done.2
  131.7 0.0 collective-permute-done.3
  131.7 1.9 pad_maximum_fusion
  133.7 64.8 %gather_fusion.5 = bf16[16384,256]{1,0:T(8,128)(2,1)} fusion(bf16[5120,256]{1,0:T(8,128)(2,1)S(1)} %pad_maximum_fusion, s32[16384]{0:T(1024)S(1)} %broadcast_clamp_fusion), kind=kCustom, calls=%fused_computation.5 | custom fusion | bytes 16842752 | tf_op jit(solution)/shard_map/gather | solution.py:8
  198.5 15.0 %reshape.153 = f32[4096,4,256]{2,1,0:T(4,128)} reshape(bf16[16384,256]{1,0:T(8,128)(2,1)} %gather_fusion.5) | data formatting | bytes 25165824 | tf_op jit(solution)/shard_map/convert_element_type | solution.py:8
  213.5 0.0 copy-done.1
  213.5 0.0 copy-start.13
  213.5 24.1 %multiply_reduce_fusion = bf16[4096,256]{1,0:T(8,128)(2,1)S(1)} fusion(f32[4096,4,256]{2,1,0:T(4,128)} %reshape.153, f32[4096,4]{1,0:T(8,128)S(1)} %copy-done.1), kind=kLoop, calls=%fused_computation.11 | loop fusion | flops 7340032 | bytes 18939904 | tf_op jit(solution)/shard_map/reduce_sum | solution.py:8
  237.7 1.3 copy-done.5
  239.0 0.7 fusion.21
  239.7 0.0 copy-start.7
  239.7 0.4 fusion.11
  240.2 0.7 convert_reduce_fusion
  240.8 69.2 %psum.29 = f32[]{:T(128)} all-reduce(f32[]{:T(128)} %get-tuple-element.6), channel_id=1, replica_groups=mesh['graph'=128] {'graph'}, use_global_device_ids=true, to_apply=%region_8.0 | all-reduce | flops 1 | bytes 8 | tf_op jit(solution)/shard_map/psum | solution.py:14
  310.0 0.6 convert_divide_fusion
  310.7 0.8 fusion.16
  311.5 7.5 %mul.58 = f32[4096,4,256]{2,1,0:T(4,128)} broadcast(f32[4096,256]{1,0:T(8,128)S(1)} %fusion.16), dimensions={0,2} | broadcast | bytes 20971520 | tf_op jit(solution)/shard_map/mul | solution.py:45
  318.9 19.4 %mul.59 = f32[16384,256]{1,0:T(8,128)} reshape(f32[4096,4,256]{2,1,0:T(4,128)} %mul.58) | data formatting | bytes 33554432 | tf_op jit(solution)/shard_map/mul | solution.py:45
  338.3 99.2 %scatter_custom_fusion = f32[5120,256]{1,0:T(8,128)} fusion(s32[16384]{0:T(1024)S(1)} %reshape.125, f32[16384,256]{1,0:T(8,128)} %mul.59, f32[16384]{0:T(1024)S(1)} %mul.54, f32[]{:T(128)} %constant.8.clone.1), kind=kCustom, calls=%fused_computation.9 | custom fusion | flops 8388608 | bytes 22085636 | tf_op jit(solution)/shard_map/scatter-add | solution.py:46
  437.5 1.3 fusion.20
  438.8 1.2 collective-permute-start.4
  439.9 0.7 collective-permute-start.5
  440.6 4.5 slice.36
  445.1 2.4 collective-permute-done.4
  447.4 7.2 %scatter_fusion = f32[4096,256]{1,0:T(8,128)} fusion(f32[4096,256]{1,0:T(8,128)} %slice.36, s32[512]{0:T(512)S(1)} %bitcast.16, f32[512,256]{1,0:T(8,128)S(1)} %collective-permute-done.4), kind=kCustom, calls=%fused_computation.7 | custom fusion | flops 131072 | bytes 1574912 | tf_op jit(solution)/shard_map/scatter-add | solution.py:49
  454.6 0.0 collective-permute-done.5
  454.6 7.3 %scatter_fusion.1 = f32[4096,256]{1,0:T(8,128)} fusion(f32[4096,256]{1,0:T(8,128)} %scatter_fusion, s32[512]{0:T(512)S(1)} %bitcast.14, f32[512,256]{1,0:T(8,128)S(1)} %collective-permute-done.5), kind=kCustom, calls=%fused_computation.8 | custom fusion | flops 131072 | bytes 1574912 | tf_op jit(solution)/shard_map/scatter-add | solution.py:49
  461.9 0.0 copy-done.4
  461.9 4.9 fusion.5
  466.8 0.0 all-reduce.3.cloned.1.call-update
  466.8 0.0 copy-done.6
  466.9 1.6 fusion.7
  468.5 67.9 %all-reduce = (f32[]{:T(128)}, f32[256,47]{0,1:T(8,128)}) all-reduce(f32[]{:T(128)} %get-tuple-element.7, f32[256,47]{0,1:T(8,128)S(1)} %fusion.7), channel_id=1, replica_groups=mesh['graph'=128] {'graph'}, use_global_device_ids=true, to_apply=%region_6.0 | all-reduce | flops 12033 | bytes 96264 | tf_op jit(solution)/shard_map/psum | solution.py:16
  537.7 76.2 %all-reduce.3.cloned.1.call-done = f32[100,256]{1,0:T(8,128)} async-done(((f32[100,256]{1,0:T(8,128)}), f32[100,256]{1,0:T(8,128)}) %all-reduce.3.cloned.1.call-update) | async-done | bytes 102416 | tf_op jit(solution)/shard_map/psum | solution.py:51
  613.9 1.5 copy.27
  (21 shorter events, 0.1 us)
Async XLA Ops:
  7.2 8.9 %copy-start.8 = (s32[4096,4]{0,1:T(4,128)S(1)}, s32[4096,4]{0,1:T(4,128)}, u32[]{:S(2)}) copy-start(s32[4096,4]{0,1:T(4,128)} %param.14) | copy-start | bytes 196612
  7.2 606.7 %all-reduce.3.cloned.1.call-start = ((), (), s32[]{:S(2)}) async-start(), calls=%async_computation | async-start | bytes 212992 | tf_op jit(solution)/shard_map/psum | solution.py:51
  8.0 10.4 %copy-start.12 = (f32[4096,4]{0,1:T(4,128)S(1)}, f32[4096,4]{0,1:T(4,128)}, u32[]{:S(2)}) copy-start(f32[4096,4]{0,1:T(4,128)} %param.15) | copy-start | bytes 196612
  9.7 7.1 %copy-start.2 = (bf16[4096,100]{1,0:T(8,128)(2,1)}, bf16[4096,100]{1,0:T(8,128)(2,1)S(1)}, u32[]{:S(2)}) copy-start(bf16[4096,100]{1,0:T(8,128)(2,1)S(1)} %copy.18) | copy-start | bytes 2457604
  11.6 7.5 %collective-permute-start = (bf16[512,100]{1,0:T(8,128)(2,1)}, bf16[512,100]{1,0:T(8,128)(2,1)}, u32[]{:S(2)}, u32[]{:S(2)}) collective-permute-start(bf16[512,100]{1,0:T(8,128)(2,1)} %gather_fusion), channel_id=1, source_target_pairs={{0,127},{1,0},{2,1},{3,2},{4,3},{5,4},{6,5},{7,6},{8,7},{9,8},{10,... | collective-permute-start | bytes 307208 | tf_op jit(solution)/shard_map/ppermute | solution.py:31
  14.8 9.1 %collective-permute-start.1 = (bf16[512,100]{1,0:T(8,128)(2,1)}, bf16[512,100]{1,0:T(8,128)(2,1)}, u32[]{:S(2)}, u32[]{:S(2)}) collective-permute-start(bf16[512,100]{1,0:T(8,128)(2,1)} %gather_fusion.1), channel_id=1, source_target_pairs={{0,1},{1,2},{2,3},{3,4},{4,5},{5,6},{6,7},{7,8},{8,9},{9,10},{10,1... | collective-permute-start | bytes 307208 | tf_op jit(solution)/shard_map/ppermute | solution.py:30
  19.1 107.9 %copy-start = (f32[4096,4]{1,0:T(8,128)}, f32[4096,4]{1,0:T(8,128)S(1)}, u32[]{:S(2)}) copy-start(f32[4096,4]{1,0:T(8,128)S(1)} %copy.20) | copy-start | bytes 196612
  82.9 23.6 %copy-start.10 = (f32[100,256]{1,0:T(8,128)S(1)}, f32[100,256]{1,0:T(8,128)}, u32[]{:S(2)}) copy-start(f32[100,256]{1,0:T(8,128)} %param.11) | copy-start | bytes 307204
  106.6 7.3 %copy-start.3 = (bf16[4096,100]{1,0:T(8,128)(2,1)}, bf16[4096,100]{1,0:T(8,128)(2,1)S(1)}, u32[]{:S(2)}) copy-start(bf16[4096,100]{1,0:T(8,128)(2,1)S(1)} %fusion.2) | copy-start | bytes 2457604
  117.9 13.8 %collective-permute-start.2 = (bf16[512,256]{1,0:T(8,128)(2,1)}, bf16[512,256]{1,0:T(8,128)(2,1)}, u32[]{:S(2)}, u32[]{:S(2)}) collective-permute-start(bf16[512,256]{1,0:T(8,128)(2,1)} %gather_fusion.3), channel_id=1, source_target_pairs={{0,127},{1,0},{2,1},{3,2},{4,3},{5,4},{6,5},{7,6},{8,7},{9,8},{10,... | collective-permute-start | bytes 786440 | tf_op jit(solution)/shard_map/ppermute | solution.py:31
  126.9 4.8 collective-permute-start.3
  198.5 15.0 %copy-start.1 = (f32[4096,4]{1,0:T(8,128)S(1)}, f32[4096,4]{1,0:T(8,128)}, u32[]{:S(2)}) copy-start(f32[4096,4]{1,0:T(8,128)} %copy-done) | copy-start | bytes 196612
  213.5 25.5 %copy-start.9 = (f32[256,47]{0,1:T(8,128)S(1)}, f32[256,47]{0,1:T(8,128)}, u32[]{:S(2)}) copy-start(f32[256,47]{0,1:T(8,128)} %param.12) | copy-start | bytes 144388
  213.5 26.2 %copy-start.11 = (s32[4096]{0:T(1024)S(1)}, s32[4096]{0:T(1024)}, u32[]{:S(2)}) copy-start(s32[4096]{0:T(1024)} %param.16) | copy-start | bytes 49156
  213.5 26.6 %copy-start.13 = (s32[4096]{0:T(1024)S(1)}, s32[4096]{0:T(1024)}, u32[]{:S(2)}) copy-start(s32[4096]{0:T(1024)} %param.17) | copy-start | bytes 49156
  237.7 1.3 copy-start.5
  239.7 79.2 %copy-start.7 = (f32[4096,47]{0,1:T(8,128)}, f32[4096,47]{0,1:T(8,128)S(1)}, u32[]{:S(2)}) copy-start(f32[4096,47]{0,1:T(8,128)S(1)} %get-tuple-element.17) | copy-start | bytes 2310148
  438.8 8.7 %collective-permute-start.4 = (f32[512,256]{1,0:T(8,128)S(1)}, f32[512,256]{1,0:T(8,128)S(1)}, u32[]{:S(2)}, u32[]{:S(2)}) collective-permute-start(f32[512,256]{1,0:T(8,128)S(1)} %get-tuple-element.11), channel_id=1, source_target_pairs={{0,127},{1,0},{2,1},{3,2},{4,3},{5,4},{6,5},{7,6},{8,7},{9,8},{10,... | collective-permute-start | bytes 1572872 | tf_op jit(solution)/shard_map/ppermute | solution.py:48
  439.9 14.7 %collective-permute-start.5 = (f32[512,256]{1,0:T(8,128)S(1)}, f32[512,256]{1,0:T(8,128)S(1)}, u32[]{:S(2)}, u32[]{:S(2)}) collective-permute-start(f32[512,256]{1,0:T(8,128)S(1)} %get-tuple-element.10), channel_id=1, source_target_pairs={{0,1},{1,2},{2,3},{3,4},{4,5},{5,6},{6,7},{7,8},{8,9},{9,10},{10,1... | collective-permute-start | bytes 1572872 | tf_op jit(solution)/shard_map/ppermute | solution.py:47
  454.6 7.3 %copy-start.4 = (bf16[4096,100]{1,0:T(8,128)(2,1)S(1)}, bf16[4096,100]{1,0:T(8,128)(2,1)}, u32[]{:S(2)}) copy-start(bf16[4096,100]{1,0:T(8,128)(2,1)} %copy-done.3) | copy-start | bytes 2457604
  461.9 4.9 copy-start.6
Sparse Core Ops, SparseCore 0:
  467.0 146.8 all-reduce.2
where the time goes:
time: 625 us; the launch traced here: 623 us
  local copies, waits for them, and re-layouts  194 us (31%)
  other arithmetic  168 us (27%)
  blocking collectives  137 us (22%)
  waiting for transfers between devices  83.4 us (13%)
  between operations  16.7 us (3%)
  starting transfers between devices  13.5 us (2%)
  matrix products  11.2 us (2%)
    gather x2, local copies, waits for them, and re-layouts, gather_sum(): return jnp.sum(buffer[src_rows] * weights[:, :, None], axis=1)  122 us
    scatter-add x1, other arithmetic, device_step(): jax.ops.segment_sum(contrib, edge_src.reshape(-1), num_segments=own_rows...  99.2 us
    psum x1, waiting for transfers between devices, device_step(): lax.psum(jnp.einsum('nf,nh->fh', z_one, grad_pre, preferred_element_type=...  76.2 us
    psum x1, blocking collectives, head_grads(): label_count = lax.psum(jnp.sum(mark_rows), 'graph')  69.2 us
    psum x1, blocking collectives, head_grads(): lax.psum(jnp.sum(mark_rows * (log_norm - jnp.sum(logits * onehot, axis=1)...  67.9 us
    reduce_sum x2, other arithmetic, gather_sum(): return jnp.sum(buffer[src_rows] * weights[:, :, None], axis=1)  47.8 us
    mul x2, local copies, waits for them, and re-layouts, device_step(): edge_w[:, :, None] * grad_agg[:, None, :]  26.9 us
    convert_element_type x1, local copies, waits for them, and re-layouts, gather_sum(): return jnp.sum(buffer[src_rows] * weights[:, :, None], axis=1)  15 us
  transfers between devices with their start and end apart: 7, of which 3 were waited for; matrix products, arithmetic and copies ran while one was open for 4% of the time, Pallas kernels for 0%

commit v1 on v0

v1 whole, which is shorter than its diff:
```python
import functools

import jax
import jax.numpy as jnp
from jax import lax
from jax.experimental import pallas as pl
from jax.experimental.pallas import tpu as pltpu
from jax.sharding import PartitionSpec as P

MESH = pl.DeviceIdType.MESH
F32 = jnp.float32
BF16 = jnp.bfloat16
VMEM = pl.BlockSpec(memory_space=pltpu.VMEM)
SMEM = pl.BlockSpec(memory_space=pltpu.SMEM)
ANY = pl.BlockSpec(memory_space=pl.ANY)
CLASSES = 47
LANES = 128
CHUNK = 256


def wrap(value, size):
    return lax.rem(value + size, size)


def remote(src, dst, send_sem, recv_sem, dev):
    return pltpu.make_async_remote_copy(src_ref=src, dst_ref=dst, send_sem=send_sem, recv_sem=recv_sem, device_id=(dev,), device_id_type=MESH)


def enter(peers):
    barrier = pltpu.get_barrier_semaphore()
    for dev in peers:
        pl.semaphore_signal(barrier, inc=1, device_id=(dev,), device_id_type=MESH)


def entered(peers):
    pl.semaphore_wait(pltpu.get_barrier_semaphore(), len(peers))


def line_peers(me):
    block, in_x = me // 8, lax.rem(me, 8)
    plane, in_y = me // 32, lax.rem(block, 4)
    along_x = [block * 8 + lax.rem(in_x + d, 8) for d in range(1, 8)]
    along_y = [plane * 32 + lax.rem(in_y + d, 4) * 8 + in_x for d in range(1, 4)]
    along_z = [lax.rem(plane + d, 4) * 32 + in_y * 8 + in_x for d in range(1, 4)]
    return in_x, in_y, plane, along_x, along_y, along_z


def spread(slots, mine, peers, send_sem, recv_sem):
    copies = []
    for d, dev in enumerate(peers):
        copies.append(remote(slots.at[mine], slots.at[mine], send_sem.at[d], recv_sem.at[d], dev))
        copies[-1].start()
    return copies


def settle(copies):
    for copy in copies:
        copy.wait()


def slot_sum(slots):
    total = slots[0]
    for i in range(1, slots.shape[0]):
        total = total + slots[i]
    return total


def pick_rows(send_idx, src, stage, halo):
    for side in range(2):
        for j in range(halo):
            stage[pl.ds(side * halo + j, 1), :] = src[pl.ds(send_idx[side, j], 1), :]


def feats_kernel(halo, send_idx, feats_t, mask, x_out, send_buf, count_out, wide, stage):
    feats, own = feats_t.shape
    mask_f = mask[...].astype(F32)
    count_out[...] = functools.reduce(lambda a, b: a + b, [mask_f[8 * i:8 * i + 8] for i in range(mask.shape[0] // 8)])
    wide[pl.ds(0, feats), :] = feats_t[...].astype(F32)
    wide[pl.ds(feats, LANES - feats), :] = jnp.zeros((LANES - feats, own), F32)
    for b in range(own // LANES):
        x_out[pl.ds(b * LANES, LANES), :] = wide[:, b * LANES:(b + 1) * LANES].T
    pick_rows(send_idx, x_out, stage, halo)
    send_buf[...] = stage[...].astype(BF16)


def swap_kernel(halo, num_parts, send_buf, count_in, recv_buf, count_out, counts, sem_s, sem_r, csem_s, csem_r):
    me = lax.axis_index('graph')
    nxt, prv = wrap(me + 1, num_parts), wrap(me - 1, num_parts)
    in_x, _, _, along_x, _, _ = line_peers(me)
    peers = [nxt, prv] + along_x
    enter(peers)
    counts[in_x] = count_in[...]
    entered(peers)
    copies = [remote(send_buf.at[pl.ds(0, halo)], recv_buf.at[pl.ds(halo, halo)], sem_s.at[0], sem_r.at[0], nxt),
              remote(send_buf.at[pl.ds(halo, halo)], recv_buf.at[pl.ds(0, halo)], sem_s.at[1], sem_r.at[1], prv)]
    for copy in copies:
        copy.start()
    settle(spread(counts, in_x, along_x, csem_s, csem_r))
    count_out[...] = slot_sum(counts)
    settle(copies)


def hidden_kernel(halo, num_parts, send_buf, count_in, recv_buf, count_out, count_y, count_z, sem_s, sem_r, csem_s, csem_r):
    me = lax.axis_index('graph')
    nxt, prv = wrap(me + 1, num_parts), wrap(me - 1, num_parts)
    _, in_y, in_z, _, along_y, along_z = line_peers(me)
    peers = [nxt, prv] + along_y + along_z
    enter(peers)
    count_y[in_y] = count_in[...]
    entered(peers)
    copies = [remote(send_buf.at[pl.ds(0, halo)], recv_buf.at[pl.ds(halo, halo)], sem_s.at[0], sem_r.at[0], nxt),
              remote(send_buf.at[pl.ds(halo, halo)], recv_buf.at[pl.ds(0, halo)], sem_s.at[1], sem_r.at[1], prv)]
    for copy in copies:
        copy.start()
    settle(spread(count_y, in_y, along_y, csem_s.at[0], csem_r.at[0]))
    count_z[in_z] = slot_sum(count_y)
    settle(spread(count_z, in_z, along_z, csem_s.at[1], csem_r.at[1]))
    count_out[...] = jnp.full(count_out.shape, jnp.sum(slot_sum(count_z)), F32)
    settle(copies)


def grads_kernel(num_parts, halo, send_buf, recv_buf, sem_s, sem_r):
    me = lax.axis_index('graph')
    nxt, prv = wrap(me + 1, num_parts), wrap(me - 1, num_parts)
    enter([nxt, prv])
    entered([nxt, prv])
    copies = [remote(send_buf.at[pl.ds(0, halo)], recv_buf.at[pl.ds(halo, halo)], sem_s.at[0], sem_r.at[0], nxt),
              remote(send_buf.at[pl.ds(halo, halo)], recv_buf.at[pl.ds(0, halo)], sem_s.at[1], sem_r.at[1], prv)]
    for copy in copies:
        copy.start()
    settle(copies)


def reduce_kernel(mine, whole, by_x, by_y, by_z, sem_s, sem_r):
    me = lax.axis_index('graph')
    in_x, in_y, in_z, along_x, along_y, along_z = line_peers(me)
    peers = along_x + along_y + along_z
    enter(peers)
    by_x[in_x] = mine[in_x]
    entered(peers)
    copies = []
    for d, dev in enumerate(along_x):
        copies.append(remote(mine.at[lax.rem(in_x + d + 1, 8)], by_x.at[in_x], sem_s.at[0, d], sem_r.at[0, d], dev))
        copies[-1].start()
    settle(copies)
    by_y[in_y] = slot_sum(by_x)
    settle(spread(by_y, in_y, along_y, sem_s.at[1], sem_r.at[1]))
    by_z[in_z] = slot_sum(by_y)
    settle(spread(by_z, in_z, along_z, sem_s.at[2], sem_r.at[2]))
    whole[in_x] = slot_sum(by_z)
    settle(spread(whole, in_x, along_x, sem_s.at[3], sem_r.at[3]))


def packed_places(feats, classes, hid):
    places, at = [], 0
    for rows in (feats, classes):
        for col in range(0, hid, LANES):
            places.append((at, rows, col))
            at += -(-rows // 8) * 8
    return places, at


def finish_kernel(whole, count, out_one, out_two, out_loss):
    feats, hid = out_one.shape
    places, at = packed_places(feats, out_two.shape[0], hid)
    half = len(places) // 2
    for ref, spots in ((out_one, places[:half]), (out_two, places[half:])):
        for start, rows, col in spots:
            ref[:, col:col + LANES] = whole[pl.ds(start, rows), :]
    out_loss[...] = jnp.full(out_loss.shape, jnp.sum(whole[pl.ds(at, 8), :]), F32) / count[...]


def columns(w3, t, *more):
    parts = [w3[t]] + [ref[t].astype(F32) for ref in more]
    parts.append(jnp.zeros((8 - 4 - len(more), LANES), F32))
    return jnp.concatenate(parts, axis=0).T


def layer_one_kernel(halo, src_any, src_v, x_any, x_halo, w3, w_one, send_idx, z_out, h_out, src_out, hsend, *scratch):
    idx, slots = scratch[0:2], (scratch[2:6], scratch[6:10])
    stage, x_buf, sem, xsem = scratch[10:14]
    own = z_out.shape[0]
    pull = pltpu.make_async_copy(x_any, x_buf.at[pl.ds(0, own)], xsem)
    pull.start()
    steps = own // CHUNK
    src_out[...] = src_v[...] * 2

    def fetch(c, b):
        return pltpu.make_async_copy(src_any.at[pl.ds(2 * c, 2)], idx[b], sem.at[b])

    def gather(b):
        for k in range(4):
            for t in range(2):
                for j in range(LANES):
                    slots[b][k][pl.ds(t * LANES + j, 1), :] = x_buf[pl.ds(idx[b][t, k, j], 1), :]

    def dense(c, b):
        r0 = pl.multiple_of(c * CHUNK, CHUNK)
        blocks = []
        for t in range(2):
            cols = columns(w3, 2 * c + t)
            sl = pl.ds(t * LANES, LANES)
            acc = slots[b][0][sl, :] * cols[:, 0:1]
            for k in range(1, 4):
                acc = acc + slots[b][k][sl, :] * cols[:, k:k + 1]
            blocks.append(acc.astype(BF16))
        z = jnp.concatenate(blocks, axis=0)
        z_out[pl.ds(r0, CHUNK), :] = z
        y = jnp.dot(z, w_one[...], preferred_element_type=F32)
        h = jnp.maximum(y, 0.0).astype(BF16).astype(F32)
        h_out[pl.ds(2 * r0, CHUNK, stride=2), :] = h[:, :LANES]
        h_out[pl.ds(2 * r0 + 1, CHUNK, stride=2), :] = h[:, LANES:]

    for b in range(2):
        fetch(b, b).start()
    for k in range(4):
        slots[1][k][...] = jnp.zeros(slots[1][k].shape, F32)
    x_buf[pl.ds(own, 2 * halo), :] = x_halo[...].astype(F32)
    pull.wait()

    def body(g, carry):
        for b in range(2):
            c = g * 2 + b
            fetch(c, b).wait()
            gather(b)
            dense(jnp.maximum(c - 1, 0), 1 - b)

            @pl.when(c + 2 < steps)
            def _():
                fetch(c + 2, b).start()
        return carry

    lax.fori_loop(0, steps // 2, body, 0)
    dense(steps - 1, 1)
    for side in range(2):
        for j in range(halo):
            i = pl.multiple_of(send_idx[side, j] * 2, 2)
            stage[pl.ds(2 * (side * halo + j), 2), :] = h_out[pl.ds(i, 2), :]
    hsend[...] = stage[...].astype(BF16)


def layer_two_kernel(src_any, src2_any, h_any, h_halo, w3, labels, mask, w_two, count, p_out, grad_two, loss, *scratch):
    fwd_idx, bwd_idx = scratch[0:2], scratch[2:4]
    slots = (scratch[4:8], scratch[8:12])
    terms = (scratch[12:16], scratch[16:20])
    sums = scratch[20:28]
    h_buf, fsem, bsem, hsem = scratch[28:32]
    own = w3.shape[0] * LANES
    steps = own // CHUNK
    pull = pltpu.make_async_copy(h_any, h_buf.at[pl.ds(0, 2 * own)], hsem)
    pull.start()

    def fetch(c, b):
        return pltpu.make_async_copy(src2_any.at[pl.ds(2 * c, 2)], fwd_idx[b], fsem.at[b])

    def refetch(c, b):
        return pltpu.make_async_copy(src_any.at[pl.ds(2 * c, 2)], bwd_idx[b], bsem.at[b])

    def gather(b):
        for k in range(4):
            for t in range(2):
                for j in range(LANES):
                    i = pl.multiple_of(fwd_idx[b][t, k, j], 2)
                    slots[b][k][pl.ds(2 * (t * LANES + j), 2), :] = h_buf[pl.ds(i, 2), :]

    def dense(c, b, valid):
        zs, lab, scale, marks = [], [], [], []
        cols_t = []
        for t in range(2):
            cols = columns(w3, 2 * c + t, labels, mask)
            cols_t.append(cols)
            halves = []
            for half in range(2):
                sl = pl.ds(2 * t * LANES + half, LANES, stride=2)
                acc = slots[b][0][sl, :] * cols[:, 0:1]
                for k in range(1, 4):
                    acc = acc + slots[b][k][sl, :] * cols[:, k:k + 1]
                halves.append(acc.astype(BF16))
            zs.append(jnp.concatenate(halves, axis=1))
        z = jnp.concatenate(zs, axis=0)
        logits = jnp.dot(z, w_two[...], preferred_element_type=F32)
        lane = lax.broadcasted_iota(jnp.int32, (CHUNK, LANES), 1)
        lab = jnp.concatenate([cols[:, 4:5] for cols in cols_t], axis=0).astype(jnp.int32)
        marks = jnp.where(valid, jnp.concatenate([cols[:, 5:6] for cols in cols_t], axis=0), 0.0)
        hot = lane == lab
        shown = jnp.where(lane < CLASSES, logits, -1e30)
        top = jnp.max(shown, axis=1, keepdims=True)
        expo = jnp.exp(shown - top)
        norm = jnp.sum(expo, axis=1, keepdims=True)
        picked = jnp.sum(jnp.where(hot, logits, 0.0), axis=1, keepdims=True)
        row_loss = marks * (jnp.log(norm) + top - picked)
        loss[...] += jnp.full(loss.shape, jnp.sum(row_loss), F32) * first_cell
        grad = ((expo / norm - jnp.where(hot, 1.0, 0.0)) * (marks / count[0, 0])).astype(BF16)
        grad_two[...] += lax.dot_general(grad, z, (((0,), (0,)), ((), ())), preferred_element_type=F32)
        wide = grad.astype(F32)
        for t in range(2):
            sl = pl.ds(t * LANES, LANES)
            for k in range(4):
                terms[b][k][sl, :] = wide[t * LANES:(t + 1) * LANES] * cols_t[t][:, k:k + 1]

    def scatter(b):
        for t in range(2):
            for j in range(0, LANES, 2):
                where, had = [], []
                for u in range(2):
                    for k in range(4):
                        where.append(pl.ds(bwd_idx[b][t, k, j + u], 1))
                for u in range(2):
                    for k in range(4):
                        had.append(sums[4 * u + k][where[4 * u + k], :] + terms[b][k][pl.ds(t * LANES + j + u, 1), :])
                for u in range(2):
                    for k in range(4):
                        sums[4 * u + k][where[4 * u + k], :] = had[4 * u + k]

    cell = (lax.broadcasted_iota(jnp.int32, loss.shape, 0) == 0) & (lax.broadcasted_iota(jnp.int32, loss.shape, 1) == 0)
    first_cell = jnp.where(cell, 1.0, 0.0).astype(F32)
    for b in range(2):
        fetch(b, b).start()
        refetch(0, b).start()
    for acc in sums:
        acc[...] = jnp.zeros(acc.shape, F32)
    for k in range(4):
        slots[1][k][...] = jnp.zeros(slots[1][k].shape, F32)
        for b in range(2):
            terms[b][k][...] = jnp.zeros(terms[b][k].shape, F32)
    loss[...] = jnp.zeros(loss.shape, F32)
    grad_two[...] = jnp.zeros(grad_two.shape, F32)
    h_buf[pl.ds(2 * own, h_halo.shape[0]), :] = h_halo[...].astype(F32)
    pull.wait()

    def body(g, carry):
        for b in range(2):
            c = g * 2 + b
            fetch(c, b).wait()
            refetch(c, b).wait()
            gather(b)
            dense(jnp.maximum(c - 1, 0), 1 - b, c > 0)
            scatter(b)
            refetch(c, b).start()

            @pl.when(c + 2 < steps)
            def _():
                fetch(c + 2, b).start()
        return carry

    lax.fori_loop(0, steps // 2, body, 0)
    refetch(steps - 2, 0).wait()
    dense(steps - 1, 1, True)
    scatter(0)
    refetch(steps - 1, 1).wait()
    scatter(1)
    p_out[...] = functools.reduce(lambda a, b: a + b, [acc[...] for acc in sums])


def layer_one_grad_kernel(halo, feats, classes, send_idx, p_buf, back, z_one, h_any, w_stack, grad_two, loss, packed, grad_one, p_own, h_buf, sem):
    own = z_one.shape[0]
    pull = pltpu.make_async_copy(h_any, h_buf, sem)
    pull.start()
    p_own[...] = p_buf[pl.ds(0, own), :]
    for side in range(2):
        for j in range(0, halo, 16):
            rows = [send_idx[side, j + u] for u in range(16)]
            new = [p_own[pl.ds(rows[u], 1), :] + back[pl.ds(side * halo + j + u, 1), :] for u in range(16)]
            for u in range(16):
                p_own[pl.ds(rows[u], 1), :] = new[u]
    grad_one[...] = jnp.zeros(grad_one.shape, F32)
    pull.wait()

    def body(c, carry):
        r0 = pl.multiple_of(c * CHUNK, CHUNK)
        p = p_own[pl.ds(r0, CHUNK), :]
        high = p.astype(BF16)
        rest = p - high.astype(F32)
        mid = rest.astype(BF16)
        low = (rest - mid.astype(F32)).astype(BF16)
        both = high.astype(F32) + pltpu.roll(mid.astype(F32), 64, 1)
        lhs = jnp.concatenate([both.astype(BF16), low], axis=1)
        hidden = jnp.dot(lhs, w_stack[...], preferred_element_type=F32)
        h = jnp.concatenate([h_buf[pl.ds(2 * r0 + half, CHUNK, stride=2), :] for half in range(2)], axis=1)
        grad = jnp.where(h > 0, hidden, 0.0).astype(BF16)
        grad_one[...] += lax.dot_general(z_one[pl.ds(r0, CHUNK), :], grad, (((0,), (0,)), ((), ())), preferred_element_type=F32)
        return carry

    lax.fori_loop(0, own // CHUNK, body, 0)
    places, at = packed_places(feats, classes, grad_one.shape[1])
    half = len(places) // 2
    for ref, spots in ((grad_one, places[:half]), (grad_two, places[half:])):
        for start, rows, col in spots:
            rows = -(-rows // 8) * 8
            packed[pl.ds(start, rows), :] = ref[pl.ds(0, rows), col:col + LANES]
    packed[pl.ds(at, 8), :] = loss[...]
    packed[pl.ds(at + 8, packed.shape[0] - at - 8), :] = jnp.zeros((packed.shape[0] - at - 8, LANES), F32)


def params(mib, collective_id=None):
    if collective_id is None:
        return pltpu.CompilerParams(vmem_limit_bytes=mib * 2 ** 20)
    return pltpu.CompilerParams(vmem_limit_bytes=mib * 2 ** 20, collective_id=collective_id, has_side_effects=True)


def solution(mesh):
    num_parts = mesh.shape['graph']
    row_spec = P('graph', None)

    def device_step(node_feats, w_one, w_two, send_idx, edge_src, edge_w, labels, label_mask):
        own, feats = node_feats.shape
        hid, classes = w_two.shape
        halo = send_idx.shape[1] // 2
        blocks = own // LANES
        buf = own + 2 * halo
        dma = pltpu.SemaphoreType.DMA
        shape = jax.ShapeDtypeStruct
        src3 = edge_src.T.reshape(4, blocks, LANES).transpose(1, 0, 2)
        w3 = edge_w.T.reshape(4, blocks, LANES).transpose(1, 0, 2)
        labels3 = labels.reshape(blocks, 1, LANES)
        mask3 = label_mask.reshape(blocks, 1, LANES)
        w_one_b = jnp.pad(w_one.astype(BF16), ((0, LANES - feats), (0, 0)))
        w_two_b = jnp.pad(w_two.astype(BF16), ((0, 0), (0, LANES - classes)))
        w_two_t = jnp.pad(w_two.astype(BF16).T, ((0, 64 - classes), (0, 0)))
        w_stack = jnp.concatenate([w_two_t, w_two_t, w_two_t, jnp.zeros_like(w_two_t)], axis=0)
        tile = shape((8, LANES), F32)

        x_own, x_send, count_own = pl.pallas_call(
            functools.partial(feats_kernel, halo), name='feats',
            out_shape=(shape((own, LANES), F32), shape((2 * halo, LANES), BF16), tile),
            in_specs=[SMEM, VMEM, VMEM], out_specs=[VMEM] * 3,
            scratch_shapes=[pltpu.VMEM((LANES, own), F32), pltpu.VMEM((2 * halo, LANES), F32)],
            compiler_params=params(16),
        )(send_idx, node_feats.T, label_mask.reshape(blocks, LANES))

        x_halo, count_x = pl.pallas_call(
            functools.partial(swap_kernel, halo, num_parts), name='swap_feats',
            out_shape=(shape((2 * halo, LANES), BF16), tile),
            in_specs=[VMEM, VMEM], out_specs=[VMEM, VMEM],
            scratch_shapes=[pltpu.VMEM((8, 8, LANES), F32), dma((2,)), dma((2,)), dma((7,)), dma((7,))],
            compiler_params=params(4, 0),
        )(x_send, count_own)

        chunk_idx = pltpu.SMEM((2, 4, LANES), jnp.int32)
        z_one, h_two, src2, h_send = pl.pallas_call(
            functools.partial(layer_one_kernel, halo), name='layer_one',
            out_shape=(shape((own, LANES), BF16), shape((2 * own, LANES), F32), shape(src3.shape, jnp.int32), shape((4 * halo, LANES), BF16)),
            in_specs=[ANY, VMEM, ANY, VMEM, VMEM, VMEM, SMEM], out_specs=[VMEM] * 4,
            scratch_shapes=[chunk_idx] * 2 + [pltpu.VMEM((CHUNK, LANES), F32)] * 8 + [pltpu.VMEM((4 * halo, LANES), F32), pltpu.VMEM((buf, LANES), F32), dma((2,)), dma],
            compiler_params=params(24),
        )(src3, src3, x_own, x_halo, w3, w_one_b, send_idx)

        h_halo, count = pl.pallas_call(
            functools.partial(hidden_kernel, 2 * halo, num_parts), name='hidden',
            out_shape=(shape((4 * halo, LANES), BF16), tile),
            in_specs=[VMEM, VMEM], out_specs=[VMEM, VMEM],
            scratch_shapes=[pltpu.VMEM((4, 8, LANES), F32)] * 2 + [dma((2,)), dma((2,)), dma((2, 3)), dma((2, 3))],
            compiler_params=params(8, 1),
        )(h_send, count_x)

        p_buf, grad_two, loss = pl.pallas_call(
            layer_two_kernel, name='layer_two',
            out_shape=(shape((buf, LANES), F32), shape((LANES, hid), F32), tile),
            in_specs=[ANY, ANY, ANY] + [VMEM] * 6, out_specs=[VMEM] * 3,
            scratch_shapes=[chunk_idx] * 4 + [pltpu.VMEM((2 * CHUNK, LANES), F32)] * 8 + [pltpu.VMEM((CHUNK, LANES), F32)] * 8 + [pltpu.VMEM((buf, LANES), F32)] * 8 + [pltpu.VMEM((2 * buf, LANES), F32), dma((2,)), dma((2,)), dma],
            compiler_params=params(48),
        )(src3, src2, h_two, h_halo, w3, labels3, mask3, w_two_b, count)

        back = pl.pallas_call(
            functools.partial(grads_kernel, num_parts, halo), name='grads',
            out_shape=shape((2 * halo, LANES), F32),
            in_specs=[VMEM], out_specs=VMEM,
            scratch_shapes=[dma((2,)), dma((2,))],
            compiler_params=params(8, 2),
        )(p_buf[own:])

        rows = packed_places(feats, classes, hid)[1] + 8
        part = -(-rows // 64) * 8
        packed = pl.pallas_call(
            functools.partial(layer_one_grad_kernel, halo, feats, classes), name='layer_one_grad',
            out_shape=shape((8 * part, LANES), F32),
            in_specs=[SMEM, VMEM, VMEM, VMEM, ANY, VMEM, VMEM, VMEM], out_specs=VMEM,
            scratch_shapes=[pltpu.VMEM((LANES, hid), F32), pltpu.VMEM((own, LANES), F32), pltpu.VMEM((2 * own, LANES), F32), dma],
            compiler_params=params(24),
        )(send_idx, p_buf, back, z_one, h_two, w_stack, grad_two, loss)

        whole = pl.pallas_call(
            reduce_kernel, name='reduce',
            out_shape=shape((8, part, LANES), F32),
            in_specs=[VMEM], out_specs=VMEM,
            scratch_shapes=[pltpu.VMEM((8, part, LANES), F32), pltpu.VMEM((4, part, LANES), F32), pltpu.VMEM((4, part, LANES), F32), dma((4, 7)), dma((4, 7))],
            compiler_params=params(4, 3),
        )(packed.reshape(8, part, LANES))

        out_one, out_two, out_loss = pl.pallas_call(
            finish_kernel, name='finish',
            out_shape=(shape((feats, hid), F32), shape((classes, hid), F32), tile),
            in_specs=[VMEM] * 2, out_specs=[VMEM] * 3,
            compiler_params=params(4),
        )(whole.reshape(8 * part, LANES), count)
        return out_loss[0, 0], out_one, out_two.T

    mapped = jax.shard_map(device_step, mesh=mesh, in_specs=(row_spec, P(), P(), row_spec, row_spec, row_spec, P('graph'), P('graph')), out_specs=(P(), P(), P()), check_vma=False)

    def program(node_feats, w_one, w_two, send_idx, edge_src, edge_w, halo_src, halo_w, labels, label_mask):
        return mapped(node_feats, w_one, w_two, send_idx, edge_src, edge_w, labels, label_mask)

    return program
```

time: 625 us -> 130 us (0.21)
  local copies, waits for them, and re-layouts: 194 us -> 7.7 us
  other arithmetic: 168 us -> 1.02 us
  blocking collectives: 137 us -> 0 us
  Pallas kernels: 0 us -> 120 us
  waiting for transfers between devices: 83.4 us -> 0 us
  between operations: 16.7 us -> 0.86 us
  starting transfers between devices: 13.5 us -> 0 us
  matrix products: 11.2 us -> 0 us
    psum x2 -> x0, blocking collectives: 137 us -> none  [the longest x1 69.2 us: head_grads(): label_count = lax.psum(jnp.sum(mark_rows), 'graph')]
    gather x6 -> x0, local copies, waits for them, and re-layouts: 134 us -> none  [the longest x2 122 us: gather_sum(): return jnp.sum(buffer[src_rows] * weights[:, :, None], axis=1)]
    pallas_call x0 -> x9, Pallas kernels: none -> 120 us  [the longest x1 34.8 us: device_step(): pl.pallas_call(layer_two_kernel, name='layer_two', out_shape=(shape((buf,...]
    scatter-add x3 -> x0, other arithmetic: 114 us -> none  [the longest x1 99.2 us: device_step(): jax.ops.segment_sum(contrib, edge_src.reshape(-1), num_segments=own_rows...]
    psum x1 -> x0, waiting for transfers between devices: 76.2 us -> none  [device_step(): lax.psum(jnp.einsum('nf,nh->fh', z_one, grad_pre, preferred_element_type=...]
    reduce_sum x4 -> x0, other arithmetic: 48.9 us -> none  [the longest x2 47.8 us: gather_sum(): return jnp.sum(buffer[src_rows] * weights[:, :, None], axis=1)]
    mul x3 -> x0, local copies, waits for them, and re-layouts: 28.5 us -> none  [the longest x2 26.9 us: device_step(): edge_w[:, :, None] * grad_agg[:, None, :]]
    convert_element_type x1 -> x0, local copies, waits for them, and re-layouts: 15 us -> none  [gather_sum(): return jnp.sum(buffer[src_rows] * weights[:, :, None], axis=1)]
  transfers between devices with their start and end apart: 7 -> 0, of which waited for: 3 -> 0; matrix products, arithmetic and copies ran while one was open for 4% -> 0% of each run, Pallas kernels for 0% -> 0%
where the time goes in v1:
time: 130 us
  Pallas kernels  120 us (92%)
  local copies, waits for them, and re-layouts  7.7 us (6%)
    pallas_call x1, Pallas kernels, device_step(): pl.pallas_call(layer_two_kernel, name='layer_two', out_shape=(shape((buf,...  34.8 us
    pallas_call x1, Pallas kernels, device_step(): pl.pallas_call(reduce_kernel, name='reduce', out_shape=shape((8, part, LA...  23.3 us
    pallas_call x1, Pallas kernels, device_step(): pl.pallas_call(functools.partial(layer_one_kernel, halo), name='layer_one...  18.6 us
    pallas_call x1, Pallas kernels, device_step(): pl.pallas_call(functools.partial(grads_kernel, num_parts, halo), name='gr...  11.4 us
    pallas_call x1, Pallas kernels, device_step(): pl.pallas_call(functools.partial(swap_kernel, halo, num_parts), name='swa...  10.7 us
    pallas_call x1, Pallas kernels, device_step(): pl.pallas_call(functools.partial(hidden_kernel, 2 * halo, num_parts), nam...  10.1 us
    pallas_call x1, Pallas kernels, device_step(): pl.pallas_call(functools.partial(layer_one_grad_kernel, halo, feats, clas...  8.8 us
    unnamed x29, local copies, waits for them, and re-layouts  7.04 us

profile of v1, /device:TPU:1, one launch (start us, length us, event | category | flops | bytes accessed | tf_op | source)
XLA Modules:
  0.0 129.7 jit_solution(17177686797818001529)
XLA Ops:
  0.6 0.0 copy-start.2
  0.6 1.1 copy-done.2
  1.8 0.0 copy-start.7
  1.8 0.7 copy-done.7
  2.5 0.0 copy-start.10
  2.5 0.7 copy-done.10
  3.2 0.0 copy-start.13
  3.2 0.0 copy-start.4
  3.2 0.0 copy-start.6
  3.2 0.0 copy-start.11
  3.2 0.0 copy-start.12
  3.2 1.8 %feats.1 = (f32[4096,128]{1,0:T(8,128)S(1)}, bf16[1024,128]{1,0:T(8,128)(2,1)S(1)}, f32[8,128]{1,0:T(8,128)S(1)}) custom-call(s32[2,1024]{1,0:T(2,128)S(1)} %copy-done.7, bf16[100,4096]{1,0:T(8,128)(2,1)S(1)} %bitcast.20, s32[32,128]{1,0:T(8,128)S(1)} %bitcast.28), custom_call_target="tpu_custom_call" | custom-call | tf_op jit(solution)/shard_map/feats/pallas_call | solution.py:423
  5.0 10.7 %swap_feats.1 = (bf16[1024,128]{1,0:T(8,128)(2,1)S(1)}, f32[8,128]{1,0:T(8,128)S(1)}) custom-call(bf16[1024,128]{1,0:T(8,128)(2,1)S(1)} %get-tuple-element.21.send_buf, f32[8,128]{1,0:T(8,128)S(1)} %get-tuple-element.22.count_in), custom_call_target="tpu_custom_call" | custom-call | tf_op jit(solution)/shard_map/swap_feats/pallas_call | solution.py:431
  15.7 0.9 convert_element_type.13
  16.6 0.0 copy-start.3
  16.6 0.8 copy-done.3
  17.5 0.0 copy-start.5
  17.5 0.8 copy-done.5
  18.3 0.0 copy-start.8
  18.3 0.7 copy-done.8
  19.0 18.6 %layer_one.1 = (bf16[4096,128]{1,0:T(8,128)(2,1)S(1)}, f32[8192,128]{1,0:T(8,128)S(1)}, s32[32,4,128]{2,1,0:T(4,128)S(1)}, bf16[2048,128]{1,0:T(8,128)(2,1)S(1)}) custom-call(s32[32,4,128]{2,1,0:T(4,128)S(1)} %bitcast.23, s32[32,4,128]{2,1,0:T(4,128)S(1)} %bitcast.24, f32[4096,128]{1,0:T(8,128)S(1)} %get-tuple-element.20.x_any, ...), custom_call_target="tpu_custom_call" | custom-call | tf_op jit(solution)/shard_map/layer_one/pallas_call | solution.py:440
  37.6 0.0 copy-start
  37.6 1.9 %copy-done = f32[8192,128]{1,0:T(8,128)} copy-done((f32[8192,128]{1,0:T(8,128)}, f32[8192,128]{1,0:T(8,128)S(1)}, u32[]{:S(2)}) %copy-start) | copy-done | bytes 4194328
  39.5 10.1 %hidden.1 = (bf16[2048,128]{1,0:T(8,128)(2,1)S(1)}, f32[8,128]{1,0:T(8,128)S(1)}) custom-call(bf16[2048,128]{1,0:T(8,128)(2,1)S(1)} %get-tuple-element.26.send_buf, f32[8,128]{1,0:T(8,128)S(1)} %get-tuple-element.27.count_in), custom_call_target="tpu_custom_call" | custom-call | tf_op jit(solution)/shard_map/hidden/pallas_call | solution.py:448
  49.7 0.0 copy-done.13
  49.7 0.1 copy.12
  49.9 0.0 copy-done.4
  49.9 0.0 copy-done.6
  49.9 0.0 copy-done.11
  49.9 0.0 copy-done.12
  49.9 0.0 copy-start.1
  49.9 0.0 copy-start.9
  49.9 34.8 %layer_two.1 = (f32[5120,128]{1,0:T(8,128)S(1)}, f32[128,256]{1,0:T(8,128)S(1)}, f32[8,128]{1,0:T(8,128)S(1)}) custom-call(s32[32,4,128]{2,1,0:T(4,128)S(1)} %bitcast.25, s32[32,4,128]{2,1,0:T(4,128)S(1)} %get-tuple-element.24.src2_any, f32[8192,128]{1,0:T(8,128)} %copy-done, bf16[2048,128]{1,0:T(8,128)(2,1)S(1)} %get-tuple-element.28.h_halo, ...), custom_call_target="tpu_custom_call" | custom-call | tf_op jit(solution)/shard_map/layer_two/pallas_call | solution.py:456
  84.8 11.4 %grads.1.back = f32[1024,128]{1,0:T(8,128)S(1)} custom-call(f32[1024,128]{1,0:T(8,128)S(1)} %slice.6.send_buf), custom_call_target="tpu_custom_call" | custom-call | tf_op jit(solution)/shard_map/grads/pallas_call | solution.py:464
  96.2 0.1 pad.18.clone
  96.3 0.1 maximum_maximum_fusion.w_stack
  96.4 0.0 copy-done.1
  96.4 0.0 copy-done.9
  96.4 8.8 %layer_one_grad.1 = f32[320,128]{1,0:T(8,128)S(1)} custom-call(s32[2,1024]{1,0:T(2,128)S(1)} %copy-done.9, f32[5120,128]{1,0:T(8,128)S(1)} %get-tuple-element.30.p_buf, f32[1024,128]{1,0:T(8,128)S(1)} %grads.1.back, bf16[4096,128]{1,0:T(8,128)(2,1)S(1)} %get-tuple-element.31.z_one, f32[8192,128]{1,0:T(8,128)S(1)} %copy-done.1, ...), custom_call_target="tpu_custom_call" | custom-call | tf_op jit(solution)/shard_map/layer_one_grad/pallas_call | solution.py:474
  105.2 23.3 %reduce.1 = f32[8,40,128]{2,1,0:T(8,128)S(1)} custom-call(f32[8,40,128]{2,1,0:T(8,128)S(1)} %bitcast.22), custom_call_target="tpu_custom_call" | custom-call | tf_op jit(solution)/shard_map/reduce/pallas_call | solution.py:482
  128.5 0.7 finish.1
  129.2 0.5 slice.7
  (7 shorter events, 0.1 us)
Async XLA Ops:
  0.6 1.2 copy-start.2
  1.8 0.7 copy-start.7
  2.5 0.7 copy-start.10
  3.2 46.5 %copy-start.13 = (f32[256,47]{0,1:T(8,128)S(1)}, f32[256,47]{0,1:T(8,128)}, u32[]{:S(2)}) copy-start(f32[256,47]{0,1:T(8,128)} %param.12) | copy-start | bytes 144388
  3.2 46.7 %copy-start.4 = (s32[4096,4]{0,1:T(4,128)S(1)}, s32[4096,4]{0,1:T(4,128)}, u32[]{:S(2)}) copy-start(s32[4096,4]{0,1:T(4,128)} %param.14) | copy-start | bytes 196612
  3.2 46.7 %copy-start.6 = (f32[4096,4]{0,1:T(4,128)S(1)}, f32[4096,4]{0,1:T(4,128)}, u32[]{:S(2)}) copy-start(f32[4096,4]{0,1:T(4,128)} %param.15) | copy-start | bytes 196612
  3.2 46.7 %copy-start.11 = (s32[4096]{0:T(1024)S(1)}, s32[4096]{0:T(1024)}, u32[]{:S(2)}) copy-start(s32[4096]{0:T(1024)} %param.17) | copy-start | bytes 49156
  3.2 46.7 %copy-start.12 = (s32[4096]{0:T(1024)S(1)}, s32[4096]{0:T(1024)}, u32[]{:S(2)}) copy-start(s32[4096]{0:T(1024)} %param.16) | copy-start | bytes 49156
  16.6 0.8 copy-start.3
  17.5 0.8 copy-start.5
  18.3 0.7 copy-start.8
  37.6 2.0 %copy-start = (f32[8192,128]{1,0:T(8,128)}, f32[8192,128]{1,0:T(8,128)S(1)}, u32[]{:S(2)}) copy-start(f32[8192,128]{1,0:T(8,128)S(1)} %get-tuple-element.25.h_any) | copy-start | bytes 12582916
  49.9 46.5 %copy-start.1 = (f32[8192,128]{1,0:T(8,128)S(1)}, f32[8192,128]{1,0:T(8,128)}, u32[]{:S(2)}) copy-start(f32[8192,128]{1,0:T(8,128)} %copy-done) | copy-start | bytes 12582916
  49.9 46.5 %copy-start.9 = (s32[2,1024]{1,0:T(2,128)S(1)}, s32[2,1024]{1,0:T(2,128)}, u32[]{:S(2)}) copy-start(s32[2,1024]{1,0:T(2,128)} %send_idx.5) | copy-start | bytes 24580
